TPU v7x, 32 devices: a whole 2x2x4 slice. The times are simulated.
32 devices in a mesh: slab: 2 (over y), date: 8 (over z, x), tile: 1, sub: 2 (over core).
Axes of the slice: x: 2, y: 2, z: 4, core: 2. Of those that a mesh axis runs over, the one named last changes fastest.
Arguments:
- slc: bfloat16 [2, 100, 128, 512], P(None, None, 'date', ('slab', 'tile', 'sub')), parts along dimension 3, may hold values from -300 to 300, as said below
- usable: int32 [100, 128, 512], P(None, 'date', ('slab', 'tile', 'sub')), parts along dimension 2, may hold values 0 or 1
Outputs:
- coherence: bfloat16 [2, 4, 8, 16, 128, 128], P(None, ('slab', 'tile', 'sub'), 'date'), parts along dimension 1
- linked: float32 [2, 128, 512], P(None, 'date', ('slab', 'tile', 'sub')), parts along dimension 2
There are 2 independent parts, one for each index of `slab`. A program takes and returns all parts, laid end to end along the dimension named above; each array names one. Nothing has to cross between parts.
Inputs may be any that keep to these rules, and one draw needn't show every extreme that they name: `slc`: complex samples of a partly coherent stack.
All inputs are finite; a program needn't handle non-finite values. No bound on the sum of `usable` on one device may be relied on, other than what follows from the above.
Results may differ from a plain program's by a relative error of at most 0.0016.
Values may be sent and summed in bfloat16 or wider, within the bound.
A program may use at most 64 MiB of HBM per device.

v0:
```python
import functools

import jax
import jax.numpy as jnp
from jax import lax
from jax.experimental import pallas as pl
from jax.experimental.pallas import tpu as pltpu
from jax.sharding import PartitionSpec as P

ITERS = 4
LANES = 128
PIECES = 2
NT = (((1,), (1,)), ((), ()))


def dot_nt(left, right):
    return lax.dot_general(left, right, NT, preferred_element_type=jnp.float32)


def window_coherence(real, imag, looks_count):
    dates = real.shape[0]
    plain = jnp.concatenate([real, imag], axis=1)
    swapped = jnp.concatenate([imag, -real], axis=1)
    sums = dot_nt(jnp.concatenate([plain, swapped], axis=0), plain)
    real_sum, imag_sum = sums[:dates], sums[dates:]
    rows = lax.broadcasted_iota(jnp.int32, (dates, dates), 0)
    columns = lax.broadcasted_iota(jnp.int32, (dates, dates), 1)
    diagonal = jnp.where(rows == columns, real_sum, 0.0)
    row_root = lax.rsqrt(jnp.sum(diagonal, axis=0, keepdims=True) * (1.0 / looks_count) + 1e-05)
    column_root = lax.rsqrt(jnp.sum(diagonal, axis=1, keepdims=True) * (1.0 / looks_count) + 1e-05)
    factor = column_root * row_root * (1.0 / looks_count)
    return (real_sum * factor).astype(jnp.bfloat16), (imag_sum * factor).astype(jnp.bfloat16)


def link_windows(matrices):
    dates = matrices[0].shape[1]
    row = lax.broadcasted_iota(jnp.int32, (8, dates), 0)
    is_real = row < 3
    is_imag = jnp.logical_and(row >= 3, row < 6)
    is_first = jnp.logical_or(row == 0, row == 3)
    is_second = jnp.logical_or(row == 1, row == 4)
    state = [jnp.where(is_real, 1.0, 0.0)] * len(matrices)
    result = None
    for step in range(ITERS):
        products = []
        for vec, matrix in zip(state, matrices):
            high = vec.astype(jnp.bfloat16).astype(jnp.float32)
            rest = vec - high
            middle = rest.astype(jnp.bfloat16).astype(jnp.float32)
            parts = jnp.where(is_first, high, jnp.where(is_second, middle, rest - middle))
            products.append(dot_nt(parts.astype(jnp.bfloat16), matrix))
        state, result = [], []
        for product in products:
            first, second = product[:, :dates], product[:, dates:]
            zero = jnp.zeros_like(first)
            new_real = jnp.sum(
                jnp.where(is_real, first, jnp.where(is_imag, -second, zero)), axis=0, keepdims=True
            )
            new_imag = jnp.sum(
                jnp.where(is_real, second, jnp.where(is_imag, first, zero)), axis=0, keepdims=True
            )
            power = jnp.sum(new_real * new_real + new_imag * new_imag, axis=1, keepdims=True)
            scale = lax.rsqrt(power * (1.0 / dates) + 1e-05)
            new_real = new_real * scale
            new_imag = new_imag * scale
            result.append((new_real, new_imag))
            state.append(
                jnp.where(
                    is_real,
                    jnp.broadcast_to(new_real, (8, dates)),
                    jnp.where(is_imag, jnp.broadcast_to(new_imag, (8, dates)), 0.0),
                )
            )
    return result


def send_order(count):
    middle = count // 2
    return sorted(range(1, count), key=lambda offset: (offset % 2 == 0, -abs(offset - middle), offset))


def kernel(
    count, looks_count, group,
    block_ref, coherence_ref, linked_ref,
    packed, arrived, held, vectors, turned, landed,
    send_sem, recv_sem, back_send, back_recv,
):
    me = lax.axis_index("date")
    windows = held.shape[0]
    dates = held.shape[2]
    own = dates // count
    groups = windows // group

    barrier = pltpu.get_barrier_semaphore()
    for offset in range(1, count):
        pl.semaphore_signal(
            barrier, inc=1, device_id={"date": lax.rem(me + offset, count)},
            device_id_type=pl.DeviceIdType.MESH,
        )

    order = send_order(count)

    def block_copy(part, offset):
        other = lax.rem(me + offset, count)
        return pltpu.make_async_remote_copy(
            src_ref=packed.at[other, part],
            dst_ref=arrived.at[part, me],
            send_sem=send_sem.at[part, offset],
            recv_sem=recv_sem.at[part, offset],
            device_id={"date": other},
            device_id_type=pl.DeviceIdType.MESH,
        )

    def pack(part, offset):
        other = lax.rem(me + offset, count)
        packed[other, part] = jnp.concatenate(
            [block_ref[other, part, :, side].reshape(group * own, looks_count).T for side in range(2)], axis=0
        )

    for offset in order:
        pack(0, offset)
    pl.semaphore_wait(barrier, count - 1)
    for offset in order:
        block_copy(0, offset).start()
    for part in range(1, groups):
        for offset in order:
            pack(part, offset)
        for offset in order:
            block_copy(part, offset).start()

    held[:, :, :, looks_count:] = jnp.zeros(held.shape[:3] + (held.shape[3] - looks_count,), held.dtype)

    def place_rows(part, side, source, rows):
        span = pl.ds(pl.multiple_of(source * own, own), own)
        for inner in range(group):
            held[part * group + inner, side, span, :looks_count] = rows[inner * own : (inner + 1) * own]

    def compute_part(part, carry):
        for side in range(2):
            place_rows(part, side, me, block_ref[me, part, :, side].reshape(group * own, looks_count))
        for offset in order:
            block_copy(part, offset).wait_recv()
            source = lax.rem(me + count - offset, count)
            rows = arrived[part, source].T
            for side in range(2):
                place_rows(part, side, source, rows[:, side * looks_count : (side + 1) * looks_count])
        matrices = []
        for inner in range(group):
            window = part * group + inner
            real, imag = window_coherence(held[window, 0], held[window, 1], looks_count)
            coherence_ref[0, 0, 0, window] = real
            coherence_ref[1, 0, 0, window] = imag
            matrices.append(jnp.concatenate([real, imag], axis=0))
        for inner, (real, imag) in enumerate(link_windows(matrices)):
            vectors[0, pl.ds(part * group + inner, 1)] = real
            vectors[1, pl.ds(part * group + inner, 1)] = imag
        return carry

    lax.fori_loop(0, groups, compute_part, 0)

    fold, rows, width = own // turned.shape[1], turned.shape[1], 2 * windows
    spread = jnp.concatenate([vectors[0], vectors[1]], axis=0)
    spread = jnp.pad(spread, ((0, LANES - width), (0, 0))).T.reshape(count, fold, rows, LANES)
    folded = spread[:, 0]
    for place in range(1, fold):
        folded = folded + pltpu.roll(
            spread[:, place].reshape(count * rows, LANES), place * width, 1
        ).reshape(count, rows, LANES)
    turned[...] = folded

    def back_copy(offset):
        other = lax.rem(me + offset, count)
        return pltpu.make_async_remote_copy(
            src_ref=turned.at[other],
            dst_ref=landed.at[me],
            send_sem=back_send.at[offset],
            recv_sem=back_recv.at[offset],
            device_id={"date": other},
            device_id_type=pl.DeviceIdType.MESH,
        )

    for offset in range(1, count):
        back_copy(offset).start()
    landed[me] = turned[me]
    for offset in range(1, count):
        back_copy(offset).wait_recv()
    for side in range(2):
        for place in range(fold):
            first = place * width + side * windows
            linked_ref[side, place * rows : (place + 1) * rows] = jnp.concatenate(
                [landed[source][:, first : first + windows] for source in range(count)], axis=1
            )

    def finish_part(part, carry):
        for offset in range(1, count):
            block_copy(part, offset).wait_send()
        return carry

    lax.fori_loop(0, groups, finish_part, 0)
    for offset in range(1, count):
        back_copy(offset).wait_send()


def deliver(coherence_in, linked_in, coherence_out, linked_out, sem):
    copies = [pltpu.make_async_copy(linked_in, linked_out, sem.at[0])]
    windows = coherence_in.shape[3]
    pieces = PIECES if windows % PIECES == 0 else 1
    size = windows // pieces
    for side in range(coherence_in.shape[0]):
        for piece in range(pieces):
            span = pl.ds(piece * size, size)
            copies.append(
                pltpu.make_async_copy(
                    coherence_in.at[side, :, :, span],
                    coherence_out.at[side, :, :, span],
                    sem.at[1 + side * PIECES + piece],
                )
            )
    for copy in copies:
        copy.start()
    for copy in copies:
        copy.wait()


def local(slc, usable):
    looks_count, own_dates, windows = usable.shape
    count = lax.axis_size("date")
    per_device = windows // count
    dates = own_dates * count
    masked = slc * usable.astype(jnp.bfloat16)[None]
    padded_looks = pl.cdiv(looks_count, LANES) * LANES
    group = min(per_device, max(1, LANES // own_dates))
    groups = per_device // group
    fold = max(1, own_dates // 8)
    fold = fold if own_dates % fold == 0 and 2 * per_device * fold <= LANES else 1
    blocks = jnp.transpose(
        masked.reshape(2, looks_count, own_dates, count, groups, group), (3, 4, 5, 0, 2, 1)
    )
    results = pl.pallas_call(
        functools.partial(kernel, count, looks_count, group),
        out_shape=(
            jax.ShapeDtypeStruct((2, 1, 1, per_device, dates, dates), jnp.bfloat16),
            jax.ShapeDtypeStruct((2, own_dates, windows), jnp.float32),
        ),
        in_specs=[pl.BlockSpec(memory_space=pltpu.VMEM)],
        out_specs=(
            pl.BlockSpec(memory_space=pltpu.VMEM),
            pl.BlockSpec(memory_space=pltpu.VMEM),
        ),
        scratch_shapes=[
            pltpu.VMEM((count, groups, 2 * looks_count, group * own_dates), jnp.bfloat16),
            pltpu.VMEM((groups, count, 2 * looks_count, group * own_dates), jnp.bfloat16),
            pltpu.VMEM((per_device, 2, dates, padded_looks), jnp.bfloat16),
            pltpu.VMEM((2, per_device, dates), jnp.float32),
            pltpu.VMEM((count, own_dates // fold, LANES), jnp.float32),
            pltpu.VMEM((count, own_dates // fold, LANES), jnp.float32),
            pltpu.SemaphoreType.DMA((groups, count)),
            pltpu.SemaphoreType.DMA((groups, count)),
            pltpu.SemaphoreType.DMA((count,)),
            pltpu.SemaphoreType.DMA((count,)),
        ],
        compiler_params=pltpu.CompilerParams(collective_id=0, has_side_effects=True, vmem_limit_bytes=16 << 20),
    )(blocks)
    return pl.pallas_call(
        deliver,
        out_shape=tuple(jax.ShapeDtypeStruct(array.shape, array.dtype) for array in results),
        in_specs=[pl.BlockSpec(memory_space=pl.ANY)] * 2,
        out_specs=(pl.BlockSpec(memory_space=pl.ANY),) * 2,
        scratch_shapes=[pltpu.SemaphoreType.DMA((results[0].shape[0] * PIECES + 1,))],
        compiler_params=pltpu.CompilerParams(vmem_limit_bytes=1 << 20),
    )(*results)


def solution(mesh):
    return jax.shard_map(
        local,
        mesh=mesh,
        in_specs=(
            P(None, None, "date", ("slab", "tile", "sub")),
            P(None, "date", ("slab", "tile", "sub")),
        ),
        out_specs=(
            P(None, ("slab", "tile", "sub"), "date", None, None, None),
            P(None, "date", ("slab", "tile", "sub")),
        ),
        check_vma=False,
    )
```

profile of v0, /device:TPU:0, one launch (start us, length us, event | category | flops | bytes accessed | tf_op | source)
XLA Modules:
  0.0 35.5 jit_solution(17702490499008922616)
XLA Ops:
  0.6 0.0 copy-start
  0.6 1.3 %convert_element_type.3 = bf16[100,16,128]{2,1,0:T(8,128)(2,1)S(1)} convert(s32[100,16,128]{2,1,0:T(8,128)} %param.3) | non-fusion elementwise | flops 204800 | bytes 1228800 | tf_op jit(solution)/shard_map/convert_element_type | solution.py:230
  1.9 0.1 copy-done
  2.0 0.1 broadcast_multiply_fusion
  2.1 1.4 %copy.4 = bf16[2,100,16,128]{1,2,0,3:T(8,128)(2,1)S(1)} copy(bf16[2,100,16,128]{3,2,1,0:T(8,128)(2,1)S(1)} %broadcast_multiply_fusion) | data formatting | bytes 1638400 | tf_op jit(solution)/shard_map/mul | solution.py:230
  3.5 30.9 %shard_map.41 = (bf16[2,1,1,16,128,128]{5,4,3,2,1,0:T(8,128)(2,1)S(1)}, f32[2,16,128]{2,1,0:T(8,128)S(1)}) custom-call(bf16[8,2,8,2,16,100]{5,4,3,2,1,0:T(8,128)(2,1)S(1)} %bitcast.3), custom_call_target="tpu_custom_call" | custom-call | tf_op jit(solution)/shard_map/pallas_call | solution.py:239
  34.5 1.0 %shard_map.42 = (bf16[2,1,1,16,128,128]{5,4,3,2,1,0:T(8,128)(2,1)}, f32[2,16,128]{2,1,0:T(8,128)}) custom-call(bf16[2,1,1,16,128,128]{5,4,3,2,1,0:T(8,128)(2,1)S(1)} %get-tuple-element.4.coherence_in, f32[2,16,128]{2,1,0:T(8,128)S(1)} %get-tuple-element.5.linked_in), custom_call_target="tpu_custom_call" | custom-call | tf_op jit(solution)/shard_map/pallas_call | solution.py:264
Async XLA Ops:
  0.6 1.4 %copy-start = (bf16[2,100,16,128]{3,2,1,0:T(8,128)(2,1)S(1)}, bf16[2,100,16,128]{3,2,1,0:T(8,128)(2,1)}, u32[]{:S(2)}) copy-start(bf16[2,100,16,128]{3,2,1,0:T(8,128)(2,1)} %param.2) | copy-start | bytes 2457604
where the time goes:
time: 35.6 us; the launch traced here: 35.5 us
  Pallas kernels  31.9 us (90%)
  local copies, waits for them, and re-layouts  1.52 us (4%)
  other arithmetic  1.36 us (4%)
  between operations  0.66 us (2%)
    pallas_call x1, Pallas kernels, local(): pl.pallas_call(functools.partial(kernel, count, looks_count, group), out_...  30.9 us
    mul x1, local copies, waits for them, and re-layouts, local(): masked = slc * usable.astype(jnp.bfloat16)[None]  1.42 us
    convert_element_type x1, other arithmetic, local(): masked = slc * usable.astype(jnp.bfloat16)[None]  1.28 us
    pallas_call x1, Pallas kernels, local(): pl.pallas_call(deliver, out_shape=tuple((jax.ShapeDtypeStruct(array.shape...  1.01 us

commit v1 on v0

--- a/solution.py
+++ b/solution.py
@@ -9,6 +9,7 @@
 
 ITERS = 4
 LANES = 128
+QUAD = 4
 PIECES = 2
 NT = (((1,), (1,)), ((), ()))
 
@@ -17,12 +18,34 @@
     return lax.dot_general(left, right, NT, preferred_element_type=jnp.float32)
 
 
-def window_coherence(real, imag, looks_count):
-    dates = real.shape[0]
-    plain = jnp.concatenate([real, imag], axis=1)
-    swapped = jnp.concatenate([imag, -real], axis=1)
-    sums = dot_nt(jnp.concatenate([plain, swapped], axis=0), plain)
-    real_sum, imag_sum = sums[:dates], sums[dates:]
+def lane_bit(rows, strip):
+    return (lax.broadcasted_iota(jnp.int32, (rows, LANES), 1) & strip) != 0
+
+
+def swap_strips(blocks, exact):
+    blocks = list(blocks)
+    bit, strip = len(blocks) // 2, LANES // 2
+    while bit:
+        high = lane_bit(blocks[0].shape[0], strip)
+        for low_index in range(len(blocks)):
+            if low_index & bit:
+                continue
+            first, second = blocks[low_index], blocks[low_index | bit]
+            if exact and strip != LANES // 2:
+                blocks[low_index] = jnp.where(high, pltpu.roll(second, strip, 1), first)
+                blocks[low_index | bit] = jnp.where(high, second, pltpu.roll(first, LANES - strip, 1))
+            else:
+                moved = pltpu.roll(jnp.where(high, first, second), strip, 1)
+                blocks[low_index] = jnp.where(high, moved, first)
+                blocks[low_index | bit] = jnp.where(high, second, moved)
+        bit, strip = bit // 2, strip // 2
+    return blocks
+
+
+def window_coherence(sums, looks_count):
+    dates = sums.shape[0] // 2
+    real_sum = sums[:dates, :dates] + sums[dates:, dates:]
+    imag_sum = sums[dates:, :dates] - sums[:dates, dates:]
     rows = lax.broadcasted_iota(jnp.int32, (dates, dates), 0)
     columns = lax.broadcasted_iota(jnp.int32, (dates, dates), 1)
     diagonal = jnp.where(rows == columns, real_sum, 0.0)
@@ -80,16 +103,20 @@
 
 
 def kernel(
-    count, looks_count, group,
-    block_ref, coherence_ref, linked_ref,
-    packed, arrived, held, vectors, turned, landed,
-    send_sem, recv_sem, back_send, back_recv,
+    count, looks_count, windows,
+    slc_hbm, usable_hbm, coherence_ref, linked_ref,
+    slc_ref, usable_ref, packed, arrived, vectors, turned, landed,
+    in_sem, send_sem, recv_sem, back_send, back_recv,
 ):
     me = lax.axis_index("date")
-    windows = held.shape[0]
-    dates = held.shape[2]
-    own = dates // count
-    groups = windows // group
+    own, local_windows = usable_ref.shape[1:]
+    dates = count * own
+    span = LANES // QUAD
+    full = looks_count // span
+    rest = looks_count - full * span
+    extra = packed.shape[1] - 2 * full * (windows // QUAD)
+    parts = windows // QUAD
+    tile_owners = LANES // windows
 
     barrier = pltpu.get_barrier_semaphore()
     for offset in range(1, count):
@@ -98,65 +125,111 @@
             device_id_type=pl.DeviceIdType.MESH,
         )
 
+    chunks = [(full * span, rest)] if rest else []
+    chunks += [(index * span, span) for index in range(full)]
+
+    def loads(index):
+        start, size = chunks[index]
+        looks = pl.ds(start, size)
+        return (
+            pltpu.make_async_copy(usable_hbm.at[looks], usable_ref.at[looks], in_sem.at[index, 0]),
+            pltpu.make_async_copy(slc_hbm.at[:, looks], slc_ref.at[:, looks], in_sem.at[index, 1]),
+        )
+
+    for index in range(len(chunks)):
+        for copy in loads(index):
+            copy.start()
+
+    def masked(side, look, tile):
+        lanes = slice(tile * LANES, (tile + 1) * LANES)
+        return slc_ref[side, look, :, lanes] * usable_ref[look, :, lanes].astype(jnp.float32).astype(jnp.bfloat16)
+
+    tiles = local_windows // LANES
+    for index, (start, size) in enumerate(chunks):
+        for copy in loads(index):
+            copy.wait()
+        for tile in range(tiles):
+            if size == span:
+                for side in range(2):
+                    blocks = swap_strips([masked(side, start + look, tile) for look in range(span)], False)
+                    for place, block in enumerate(blocks):
+                        owner, part = divmod(place, parts)
+                        packed[tile * tile_owners + owner, extra + (part * 2 + side) * full + start // span] = block
+            else:
+                half = tile_owners // 2
+                zero = jnp.zeros((own, LANES), jnp.bfloat16)
+                for piece in range(extra):
+                    blocks = swap_strips(
+                        [
+                            masked(side, start + piece * half + look, tile) if piece * half + look < size else zero
+                            for side in range(2)
+                            for look in range(half)
+                        ],
+                        True,
+                    )
+                    for owner, block in enumerate(blocks):
+                        packed[tile * tile_owners + owner, piece] = block
+
     order = send_order(count)
+
+    def blocks_of(part):
+        if isinstance(part, int) and part == 0:
+            return pl.ds(0, extra + 2 * full)
+        return pl.ds(extra + part * 2 * full, 2 * full)
 
     def block_copy(part, offset):
         other = lax.rem(me + offset, count)
         return pltpu.make_async_remote_copy(
-            src_ref=packed.at[other, part],
-            dst_ref=arrived.at[part, me],
+            src_ref=packed.at[other, blocks_of(part)],
+            dst_ref=arrived.at[me, blocks_of(part)],
             send_sem=send_sem.at[part, offset],
             recv_sem=recv_sem.at[part, offset],
             device_id={"date": other},
             device_id_type=pl.DeviceIdType.MESH,
         )
 
-    def pack(part, offset):
-        other = lax.rem(me + offset, count)
-        packed[other, part] = jnp.concatenate(
-            [block_ref[other, part, :, side].reshape(group * own, looks_count).T for side in range(2)], axis=0
-        )
-
-    for offset in order:
-        pack(0, offset)
     pl.semaphore_wait(barrier, count - 1)
-    for offset in order:
-        block_copy(0, offset).start()
-    for part in range(1, groups):
-        for offset in order:
-            pack(part, offset)
+    for part in range(parts):
         for offset in order:
             block_copy(part, offset).start()
-
-    held[:, :, :, looks_count:] = jnp.zeros(held.shape[:3] + (held.shape[3] - looks_count,), held.dtype)
-
-    def place_rows(part, side, source, rows):
-        span = pl.ds(pl.multiple_of(source * own, own), own)
-        for inner in range(group):
-            held[part * group + inner, side, span, :looks_count] = rows[inner * own : (inner + 1) * own]
-
-    def compute_part(part, carry):
-        for side in range(2):
-            place_rows(part, side, me, block_ref[me, part, :, side].reshape(group * own, looks_count))
+    arrived[me] = packed[me]
+
+    lane = lax.broadcasted_iota(jnp.int32, (2 * dates, LANES), 1)
+
+    def compute_part(part):
         for offset in order:
             block_copy(part, offset).wait_recv()
-            source = lax.rem(me + count - offset, count)
-            rows = arrived[part, source].T
-            for side in range(2):
-                place_rows(part, side, source, rows[:, side * looks_count : (side + 1) * looks_count])
+
+        def gathered(block):
+            return arrived[:, block].reshape(dates, LANES)
+
+        columns = []
+        for piece in range(extra):
+            both = gathered(piece)
+            columns.append((jnp.concatenate([both, pltpu.roll(both, LANES // 2, 1)], axis=0), True))
+        base = extra + part * 2 * full
+        for index in range(full):
+            columns.append((jnp.concatenate([gathered(base + index), gathered(base + full + index)], axis=0), False))
+        right = jnp.concatenate([block for block, _ in columns], axis=1)
         matrices = []
-        for inner in range(group):
-            window = part * group + inner
-            real, imag = window_coherence(held[window, 0], held[window, 1], looks_count)
+        for inner in range(QUAD):
+            window = part * QUAD + inner
+            mine = jnp.logical_and(lane < LANES // 2, (lane & (windows - 1)) == window)
+            own_lane = (lane & (QUAD - 1)) == inner
+            left = jnp.concatenate(
+                [jnp.where(mine if shared else own_lane, block, jnp.zeros_like(block)) for block, shared in columns],
+                axis=1,
+            )
+            real, imag = window_coherence(dot_nt(left, right), looks_count)
             coherence_ref[0, 0, 0, window] = real
             coherence_ref[1, 0, 0, window] = imag
             matrices.append(jnp.concatenate([real, imag], axis=0))
         for inner, (real, imag) in enumerate(link_windows(matrices)):
-            vectors[0, pl.ds(part * group + inner, 1)] = real
-            vectors[1, pl.ds(part * group + inner, 1)] = imag
-        return carry
-
-    lax.fori_loop(0, groups, compute_part, 0)
+            vectors[0, pl.ds(part * QUAD + inner, 1)] = real
+            vectors[1, pl.ds(part * QUAD + inner, 1)] = imag
+
+    for part in range(parts):
+        compute_part(part)
 
     fold, rows, width = own // turned.shape[1], turned.shape[1], 2 * windows
     spread = jnp.concatenate([vectors[0], vectors[1]], axis=0)
@@ -191,12 +264,9 @@
                 [landed[source][:, first : first + windows] for source in range(count)], axis=1
             )
 
-    def finish_part(part, carry):
+    for part in range(parts):
         for offset in range(1, count):
             block_copy(part, offset).wait_send()
-        return carry
-
-    lax.fori_loop(0, groups, finish_part, 0)
     for offset in range(1, count):
         back_copy(offset).wait_send()
 
@@ -227,40 +297,40 @@
     count = lax.axis_size("date")
     per_device = windows // count
     dates = own_dates * count
-    masked = slc * usable.astype(jnp.bfloat16)[None]
-    padded_looks = pl.cdiv(looks_count, LANES) * LANES
-    group = min(per_device, max(1, LANES // own_dates))
-    groups = per_device // group
+    parts = per_device // QUAD
+    span = LANES // QUAD
+    full = looks_count // span
+    extra = pl.cdiv(looks_count - full * span, LANES // per_device // 2)
     fold = max(1, own_dates // 8)
     fold = fold if own_dates % fold == 0 and 2 * per_device * fold <= LANES else 1
-    blocks = jnp.transpose(
-        masked.reshape(2, looks_count, own_dates, count, groups, group), (3, 4, 5, 0, 2, 1)
-    )
+    blocks = extra + 2 * full * parts
     results = pl.pallas_call(
-        functools.partial(kernel, count, looks_count, group),
+        functools.partial(kernel, count, looks_count, per_device),
         out_shape=(
             jax.ShapeDtypeStruct((2, 1, 1, per_device, dates, dates), jnp.bfloat16),
             jax.ShapeDtypeStruct((2, own_dates, windows), jnp.float32),
         ),
-        in_specs=[pl.BlockSpec(memory_space=pltpu.VMEM)],
+        in_specs=[pl.BlockSpec(memory_space=pltpu.HBM)] * 2,
         out_specs=(
             pl.BlockSpec(memory_space=pltpu.VMEM),
             pl.BlockSpec(memory_space=pltpu.VMEM),
         ),
         scratch_shapes=[
-            pltpu.VMEM((count, groups, 2 * looks_count, group * own_dates), jnp.bfloat16),
-            pltpu.VMEM((groups, count, 2 * looks_count, group * own_dates), jnp.bfloat16),
-            pltpu.VMEM((per_device, 2, dates, padded_looks), jnp.bfloat16),
+            pltpu.VMEM((2, looks_count, own_dates, windows), jnp.bfloat16),
+            pltpu.VMEM((looks_count, own_dates, windows), jnp.int32),
+            pltpu.VMEM((count, blocks, own_dates, LANES), jnp.bfloat16),
+            pltpu.VMEM((count, blocks, own_dates, LANES), jnp.bfloat16),
             pltpu.VMEM((2, per_device, dates), jnp.float32),
             pltpu.VMEM((count, own_dates // fold, LANES), jnp.float32),
             pltpu.VMEM((count, own_dates // fold, LANES), jnp.float32),
-            pltpu.SemaphoreType.DMA((groups, count)),
-            pltpu.SemaphoreType.DMA((groups, count)),
+            pltpu.SemaphoreType.DMA((full + 1, 2)),
+            pltpu.SemaphoreType.DMA((parts, count)),
+            pltpu.SemaphoreType.DMA((parts, count)),
             pltpu.SemaphoreType.DMA((count,)),
             pltpu.SemaphoreType.DMA((count,)),
         ],
-        compiler_params=pltpu.CompilerParams(collective_id=0, has_side_effects=True, vmem_limit_bytes=16 << 20),
-    )(blocks)
+        compiler_params=pltpu.CompilerParams(collective_id=0, has_side_effects=True, vmem_limit_bytes=24 << 20),
+    )(slc, usable)
     return pl.pallas_call(
         deliver,
         out_shape=tuple(jax.ShapeDtypeStruct(array.shape, array.dtype) for array in results),

time: 35.6 us -> 35.6 us (level)
  other arithmetic: 1.36 us -> 0 us
  local copies, waits for them, and re-layouts: 1.52 us -> 2.28 us
  Pallas kernels: 31.9 us -> 32.5 us
    unnamed x2 -> x4, local copies, waits for them, and re-layouts: 0.11 us -> 2.28 us
    mul x1 -> x0, local copies, waits for them, and re-layouts: 1.42 us -> none  [local(): masked = slc * usable.astype(jnp.bfloat16)[None]]
    convert_element_type x1 -> x0, other arithmetic: 1.28 us -> none  [local(): masked = slc * usable.astype(jnp.bfloat16)[None]]
    pallas_call x1, Pallas kernels: 30.9 us -> 31.5 us  [local(): pl.pallas_call(functools.partial(kernel, count, looks_count, per_device),...]
where the time goes in v1:
time: 35.6 us; the launch traced here: 35.4 us
  Pallas kernels  32.5 us (91%)
  local copies, waits for them, and re-layouts  2.28 us (6%)
  between operations  0.65 us (2%)
    pallas_call x1, Pallas kernels, local(): pl.pallas_call(functools.partial(kernel, count, looks_count, per_device),...  31.5 us
    unnamed x4, local copies, waits for them, and re-layouts  2.28 us
    pallas_call x1, Pallas kernels, local(): pl.pallas_call(deliver, out_shape=tuple((jax.ShapeDtypeStruct(array.shape...  1.01 us

profile of v1, /device:TPU:0, one launch (start us, length us, event | category | flops | bytes accessed | tf_op | source)
XLA Modules:
  0.0 35.4 jit_solution(11478943085720186360)
XLA Ops:
  0.6 0.0 copy-start
  0.6 1.1 %copy-done = bf16[2,100,16,128]{3,2,1,0:T(8,128)(2,1)S(1)} copy-done((bf16[2,100,16,128]{3,2,1,0:T(8,128)(2,1)S(1)}, bf16[2,100,16,128]{3,2,1,0:T(8,128)(2,1)}, u32[]{:S(2)}) %copy-start) | copy-done | bytes 819224
  1.8 0.0 copy-start.1
  1.8 1.1 %copy-done.1 = s32[100,16,128]{2,1,0:T(8,128)S(1)} copy-done((s32[100,16,128]{2,1,0:T(8,128)S(1)}, s32[100,16,128]{2,1,0:T(8,128)}, u32[]{:S(2)}) %copy-start.1) | copy-done | bytes 819224
  2.9 31.5 %shard_map.41 = (bf16[2,1,1,16,128,128]{5,4,3,2,1,0:T(8,128)(2,1)S(1)}, f32[2,16,128]{2,1,0:T(8,128)S(1)}) custom-call(bf16[2,100,16,128]{3,2,1,0:T(8,128)(2,1)S(1)} %copy-done, s32[100,16,128]{2,1,0:T(8,128)S(1)} %copy-done.1), custom_call_target="tpu_custom_call" | custom-call | tf_op jit(solution)/shard_map/pallas_call | solution.py:307
  34.4 1.0 %shard_map.42 = (bf16[2,1,1,16,128,128]{5,4,3,2,1,0:T(8,128)(2,1)}, f32[2,16,128]{2,1,0:T(8,128)}) custom-call(bf16[2,1,1,16,128,128]{5,4,3,2,1,0:T(8,128)(2,1)S(1)} %get-tuple-element.4.coherence_in, f32[2,16,128]{2,1,0:T(8,128)S(1)} %get-tuple-element.5.linked_in), custom_call_target="tpu_custom_call" | custom-call | tf_op jit(solution)/shard_map/pallas_call | solution.py:334
Async XLA Ops:
  0.6 1.1 %copy-start = (bf16[2,100,16,128]{3,2,1,0:T(8,128)(2,1)S(1)}, bf16[2,100,16,128]{3,2,1,0:T(8,128)(2,1)}, u32[]{:S(2)}) copy-start(bf16[2,100,16,128]{3,2,1,0:T(8,128)(2,1)} %slc_hbm.1) | copy-start | bytes 2457604
  1.8 1.1 %copy-start.1 = (s32[100,16,128]{2,1,0:T(8,128)S(1)}, s32[100,16,128]{2,1,0:T(8,128)}, u32[]{:S(2)}) copy-start(s32[100,16,128]{2,1,0:T(8,128)} %usable_hbm.1) | copy-start | bytes 2457604

commit v2 on v1

--- a/solution.py
+++ b/solution.py
@@ -63,17 +63,17 @@
     is_first = jnp.logical_or(row == 0, row == 3)
     is_second = jnp.logical_or(row == 1, row == 4)
     state = [jnp.where(is_real, 1.0, 0.0)] * len(matrices)
-    result = None
+    scales = [None] * len(matrices)
+    result = []
     for step in range(ITERS):
         products = []
         for vec, matrix in zip(state, matrices):
             high = vec.astype(jnp.bfloat16).astype(jnp.float32)
-            rest = vec - high
-            middle = rest.astype(jnp.bfloat16).astype(jnp.float32)
-            parts = jnp.where(is_first, high, jnp.where(is_second, middle, rest - middle))
-            products.append(dot_nt(parts.astype(jnp.bfloat16), matrix))
-        state, result = [], []
-        for product in products:
+            left = vec - high
+            middle = left.astype(jnp.bfloat16).astype(jnp.float32)
+            pieces = jnp.where(is_first, high, jnp.where(is_second, middle, left - middle))
+            products.append(dot_nt(pieces.astype(jnp.bfloat16), matrix))
+        for index, product in enumerate(products):
             first, second = product[:, :dates], product[:, dates:]
             zero = jnp.zeros_like(first)
             new_real = jnp.sum(
@@ -82,18 +82,19 @@
             new_imag = jnp.sum(
                 jnp.where(is_real, second, jnp.where(is_imag, first, zero)), axis=0, keepdims=True
             )
+            if step:
+                new_real = new_real * scales[index]
+                new_imag = new_imag * scales[index]
             power = jnp.sum(new_real * new_real + new_imag * new_imag, axis=1, keepdims=True)
-            scale = lax.rsqrt(power * (1.0 / dates) + 1e-05)
-            new_real = new_real * scale
-            new_imag = new_imag * scale
-            result.append((new_real, new_imag))
-            state.append(
-                jnp.where(
+            scales[index] = lax.rsqrt(power * (1.0 / dates) + 1e-05)
+            if step == ITERS - 1:
+                result.append((new_real * scales[index], new_imag * scales[index]))
+            else:
+                state[index] = jnp.where(
                     is_real,
                     jnp.broadcast_to(new_real, (8, dates)),
                     jnp.where(is_imag, jnp.broadcast_to(new_imag, (8, dates)), 0.0),
                 )
-            )
     return result
 
 
@@ -114,8 +115,9 @@
     span = LANES // QUAD
     full = looks_count // span
     rest = looks_count - full * span
-    extra = packed.shape[1] - 2 * full * (windows // QUAD)
     parts = windows // QUAD
+    extra = packed.shape[1] - 2 * full * parts
+    later = 2 * (full - 1)
     tile_owners = LANES // windows
 
     barrier = pltpu.get_barrier_semaphore()
@@ -125,8 +127,8 @@
             device_id_type=pl.DeviceIdType.MESH,
         )
 
-    chunks = [(full * span, rest)] if rest else []
-    chunks += [(index * span, span) for index in range(full)]
+    chunks = [(0, span)] + ([(full * span, rest)] if rest else [])
+    chunks += [(index * span, span) for index in range(1, full)]
 
     def loads(index):
         start, size = chunks[index]
@@ -144,8 +146,16 @@
         lanes = slice(tile * LANES, (tile + 1) * LANES)
         return slc_ref[side, look, :, lanes] * usable_ref[look, :, lanes].astype(jnp.float32).astype(jnp.bfloat16)
 
+    def first_block(part, side):
+        return 2 * part + side
+
+    def later_block(part, side, index):
+        return 2 * parts + extra + part * later + side * (full - 1) + index - 1
+
     tiles = local_windows // LANES
-    for index, (start, size) in enumerate(chunks):
+
+    def prepare(index):
+        start, size = chunks[index]
         for copy in loads(index):
             copy.wait()
         for tile in range(tiles):
@@ -154,7 +164,8 @@
                     blocks = swap_strips([masked(side, start + look, tile) for look in range(span)], False)
                     for place, block in enumerate(blocks):
                         owner, part = divmod(place, parts)
-                        packed[tile * tile_owners + owner, extra + (part * 2 + side) * full + start // span] = block
+                        row = later_block(part, side, start // span) if start else first_block(part, side)
+                        packed[tile * tile_owners + owner, row] = block
             else:
                 half = tile_owners // 2
                 zero = jnp.zeros((own, LANES), jnp.bfloat16)
@@ -168,48 +179,58 @@
                         True,
                     )
                     for owner, block in enumerate(blocks):
-                        packed[tile * tile_owners + owner, piece] = block
+                        packed[tile * tile_owners + owner, 2 * parts + piece] = block
 
     order = send_order(count)
 
-    def blocks_of(part):
-        if isinstance(part, int) and part == 0:
-            return pl.ds(0, extra + 2 * full)
-        return pl.ds(extra + part * 2 * full, 2 * full)
-
-    def block_copy(part, offset):
+    def blocks_of(message):
+        if message == 0:
+            return pl.ds(0, 2 * parts)
+        if message == 1:
+            return pl.ds(2 * parts, extra + later)
+        return pl.ds(2 * parts + extra + (message - 1) * later, later)
+
+    def block_copy(message, offset):
         other = lax.rem(me + offset, count)
         return pltpu.make_async_remote_copy(
-            src_ref=packed.at[other, blocks_of(part)],
-            dst_ref=arrived.at[me, blocks_of(part)],
-            send_sem=send_sem.at[part, offset],
-            recv_sem=recv_sem.at[part, offset],
+            src_ref=packed.at[other, blocks_of(message)],
+            dst_ref=arrived.at[me, blocks_of(message)],
+            send_sem=send_sem.at[message, offset],
+            recv_sem=recv_sem.at[message, offset],
             device_id={"date": other},
             device_id_type=pl.DeviceIdType.MESH,
         )
 
+    prepare(0)
     pl.semaphore_wait(barrier, count - 1)
-    for part in range(parts):
+    for offset in order:
+        block_copy(0, offset).start()
+    for index in range(1, len(chunks)):
+        prepare(index)
+    for message in range(1, parts + 1):
         for offset in order:
-            block_copy(part, offset).start()
+            block_copy(message, offset).start()
     arrived[me] = packed[me]
 
     lane = lax.broadcasted_iota(jnp.int32, (2 * dates, LANES), 1)
 
     def compute_part(part):
-        for offset in order:
-            block_copy(part, offset).wait_recv()
+        for message in range(0 if part == 0 else part + 1, part + 2):
+            for offset in order:
+                block_copy(message, offset).wait_recv()
 
         def gathered(block):
             return arrived[:, block].reshape(dates, LANES)
 
         columns = []
         for piece in range(extra):
-            both = gathered(piece)
+            both = gathered(2 * parts + piece)
             columns.append((jnp.concatenate([both, pltpu.roll(both, LANES // 2, 1)], axis=0), True))
-        base = extra + part * 2 * full
         for index in range(full):
-            columns.append((jnp.concatenate([gathered(base + index), gathered(base + full + index)], axis=0), False))
+            sides = [
+                gathered(later_block(part, side, index) if index else first_block(part, side)) for side in range(2)
+            ]
+            columns.append((jnp.concatenate(sides, axis=0), False))
         right = jnp.concatenate([block for block, _ in columns], axis=1)
         matrices = []
         for inner in range(QUAD):
@@ -264,9 +285,9 @@
                 [landed[source][:, first : first + windows] for source in range(count)], axis=1
             )
 
-    for part in range(parts):
+    for message in range(parts + 1):
         for offset in range(1, count):
-            block_copy(part, offset).wait_send()
+            block_copy(message, offset).wait_send()
     for offset in range(1, count):
         back_copy(offset).wait_send()
 
@@ -324,13 +345,13 @@
             pltpu.VMEM((count, own_dates // fold, LANES), jnp.float32),
             pltpu.VMEM((count, own_dates // fold, LANES), jnp.float32),
             pltpu.SemaphoreType.DMA((full + 1, 2)),
-            pltpu.SemaphoreType.DMA((parts, count)),
-            pltpu.SemaphoreType.DMA((parts, count)),
+            pltpu.SemaphoreType.DMA((parts + 1, count)),
+            pltpu.SemaphoreType.DMA((parts + 1, count)),
             pltpu.SemaphoreType.DMA((count,)),
             pltpu.SemaphoreType.DMA((count,)),
         ],
         compiler_params=pltpu.CompilerParams(collective_id=0, has_side_effects=True, vmem_limit_bytes=24 << 20),
-    )(slc, usable)
+    )(pltpu.with_memory_space_constraint(slc, pltpu.HBM), pltpu.with_memory_space_constraint(usable, pltpu.HBM))
     return pl.pallas_call(
         deliver,
         out_shape=tuple(jax.ShapeDtypeStruct(array.shape, array.dtype) for array in results),

time: 35.6 us -> 33.8 us (0.949)
  local copies, waits for them, and re-layouts: 2.28 us -> 0 us
  Pallas kernels: 32.5 us -> 33 us
    unnamed x4 -> x0, local copies, waits for them, and re-layouts: 2.28 us -> none
    pallas_call x1, Pallas kernels: 31.5 us -> 32 us  [local(): pl.pallas_call(functools.partial(kernel, count, looks_count, per_device),...]
where the time goes in v2:
time: 33.8 us; the launch traced here: 33.7 us
  Pallas kernels  33 us (98%)
  between operations  0.64 us (2%)
    pallas_call x1, Pallas kernels, local(): pl.pallas_call(functools.partial(kernel, count, looks_count, per_device),...  32 us
    pallas_call x1, Pallas kernels, local(): pl.pallas_call(deliver, out_shape=tuple((jax.ShapeDtypeStruct(array.shape...  1.01 us

profile of v2, /device:TPU:0, one launch (start us, length us, event | category | flops | bytes accessed | tf_op | source)
XLA Modules:
  0.0 33.7 jit_solution(9637417206240561361)
XLA Ops:
  0.6 32.0 %shard_map.41 = (bf16[2,1,1,16,128,128]{5,4,3,2,1,0:T(8,128)(2,1)S(1)}, f32[2,16,128]{2,1,0:T(8,128)S(1)}) custom-call(bf16[2,100,16,128]{3,2,1,0:T(8,128)(2,1)} %slc_hbm.1, s32[100,16,128]{2,1,0:T(8,128)} %usable_hbm.1), custom_call_target="tpu_custom_call" | custom-call | tf_op jit(solution)/shard_map/pallas_call | solution.py:328
  32.6 1.0 %shard_map.42 = (bf16[2,1,1,16,128,128]{5,4,3,2,1,0:T(8,128)(2,1)}, f32[2,16,128]{2,1,0:T(8,128)}) custom-call(bf16[2,1,1,16,128,128]{5,4,3,2,1,0:T(8,128)(2,1)S(1)} %get-tuple-element.4.coherence_in, f32[2,16,128]{2,1,0:T(8,128)S(1)} %get-tuple-element.5.linked_in), custom_call_target="tpu_custom_call" | custom-call | tf_op jit(solution)/shard_map/pallas_call | solution.py:355

commit v3 on v2

--- a/solution.py
+++ b/solution.py
@@ -10,6 +10,8 @@
 ITERS = 4
 LANES = 128
 QUAD = 4
+PAIR = 2
+AHEAD = 3
 PIECES = 2
 NT = (((1,), (1,)), ((), ()))
 
@@ -56,7 +58,7 @@
 
 
 def link_windows(matrices):
-    dates = matrices[0].shape[1]
+    dates = matrices[0].shape[0]
     row = lax.broadcasted_iota(jnp.int32, (8, dates), 0)
     is_real = row < 3
     is_imag = jnp.logical_and(row >= 3, row < 6)
@@ -72,15 +74,15 @@
             left = vec - high
             middle = left.astype(jnp.bfloat16).astype(jnp.float32)
             pieces = jnp.where(is_first, high, jnp.where(is_second, middle, left - middle))
-            products.append(dot_nt(pieces.astype(jnp.bfloat16), matrix))
+            products.append(jnp.dot(pieces.astype(jnp.bfloat16), matrix, preferred_element_type=jnp.float32))
         for index, product in enumerate(products):
             first, second = product[:, :dates], product[:, dates:]
             zero = jnp.zeros_like(first)
             new_real = jnp.sum(
-                jnp.where(is_real, first, jnp.where(is_imag, -second, zero)), axis=0, keepdims=True
+                jnp.where(is_real, first, jnp.where(is_imag, second, zero)), axis=0, keepdims=True
             )
             new_imag = jnp.sum(
-                jnp.where(is_real, second, jnp.where(is_imag, first, zero)), axis=0, keepdims=True
+                jnp.where(is_real, -second, jnp.where(is_imag, first, zero)), axis=0, keepdims=True
             )
             if step:
                 new_real = new_real * scales[index]
@@ -98,16 +100,30 @@
     return result
 
 
-def send_order(count):
-    middle = count // 2
-    return sorted(range(1, count), key=lambda offset: (offset % 2 == 0, -abs(offset - middle), offset))
+def descending(count, me):
+    return [top - (top <= me).astype(jnp.int32) for top in range(count - 1, 0, -1)]
+
+
+def at_distance(count, me, distance):
+    pairs = count // PAIR
+    row, side = me // PAIR, lax.rem(me, PAIR)
+    found = []
+    for across in range(PAIR):
+        steps = distance - across
+        if steps < 0:
+            continue
+        for along in sorted({steps, -steps}, reverse=True):
+            if abs(along) < pairs:
+                exists = jnp.logical_and(row + along >= 0, row + along < pairs)
+                found.append((exists, (row + along) * PAIR + (1 - side if across else side)))
+    return found
 
 
 def kernel(
     count, looks_count, windows,
     slc_hbm, usable_hbm, coherence_ref, linked_ref,
     slc_ref, usable_ref, packed, arrived, vectors, turned, landed,
-    in_sem, send_sem, recv_sem, back_send, back_recv,
+    in_sem, send_sem, recv_sem, back_send, back_recv, round_sem,
 ):
     me = lax.axis_index("date")
     own, local_windows = usable_ref.shape[1:]
@@ -121,11 +137,19 @@
     tile_owners = LANES // windows
 
     barrier = pltpu.get_barrier_semaphore()
-    for offset in range(1, count):
-        pl.semaphore_signal(
-            barrier, inc=1, device_id={"date": lax.rem(me + offset, count)},
-            device_id_type=pl.DeviceIdType.MESH,
-        )
+    farthest = count // PAIR - 1 + PAIR - 1
+    beside = at_distance(count, me, 1)
+    greetings = sum(exists.astype(jnp.int32) for exists, _ in beside)
+
+    def greet(semaphore):
+        for exists, other in beside:
+            @pl.when(exists)
+            def _():
+                pl.semaphore_signal(
+                    semaphore, inc=1, device_id={"date": other}, device_id_type=pl.DeviceIdType.MESH
+                )
+
+    greet(barrier)
 
     chunks = [(0, span)] + ([(full * span, rest)] if rest else [])
     chunks += [(index * span, span) for index in range(1, full)]
@@ -181,7 +205,7 @@
                     for owner, block in enumerate(blocks):
                         packed[tile * tile_owners + owner, 2 * parts + piece] = block
 
-    order = send_order(count)
+    others = descending(count, me)
 
     def blocks_of(message):
         if message == 0:
@@ -190,34 +214,57 @@
             return pl.ds(2 * parts, extra + later)
         return pl.ds(2 * parts + extra + (message - 1) * later, later)
 
-    def block_copy(message, offset):
-        other = lax.rem(me + offset, count)
+    def block_copy(message, other, source):
         return pltpu.make_async_remote_copy(
             src_ref=packed.at[other, blocks_of(message)],
-            dst_ref=arrived.at[me, blocks_of(message)],
-            send_sem=send_sem.at[message, offset],
-            recv_sem=recv_sem.at[message, offset],
+            dst_ref=arrived.at[source, blocks_of(message)],
+            send_sem=send_sem.at[message, other],
+            recv_sem=recv_sem.at[message, source],
             device_id={"date": other},
             device_id_type=pl.DeviceIdType.MESH,
         )
 
-    prepare(0)
-    pl.semaphore_wait(barrier, count - 1)
-    for offset in order:
-        block_copy(0, offset).start()
-    for index in range(1, len(chunks)):
-        prepare(index)
-    for message in range(1, parts + 1):
-        for offset in order:
-            block_copy(message, offset).start()
+    def send_at(distance, messages):
+        for exists, other in at_distance(count, me, distance):
+            @pl.when(exists)
+            def _():
+                for message in messages:
+                    block_copy(message, other, me).start()
+
+    def send_all(message):
+        for other in others:
+            block_copy(message, other, me).start()
+
+    with jax.named_scope("prepare_first"):
+        prepare(0)
+    with jax.named_scope("meet_first"):
+        pl.semaphore_wait(barrier, greetings)
+    if farthest > 1:
+        greet(round_sem.at[0])
+    send_at(1, [0])
+    with jax.named_scope("prepare_rest"):
+        for index in range(1, len(chunks)):
+            prepare(index)
+    send_at(1, [1])
+    for distance in range(2, farthest + 1):
+        with jax.named_scope("meet_next"):
+            pl.semaphore_wait(round_sem.at[distance - 2], greetings)
+        if distance < farthest:
+            greet(round_sem.at[distance - 1])
+        send_at(distance, [0, 1])
+    for message in range(2, min(AHEAD, parts + 1)):
+        send_all(message)
     arrived[me] = packed[me]
 
     lane = lax.broadcasted_iota(jnp.int32, (2 * dates, LANES), 1)
 
     def compute_part(part):
-        for message in range(0 if part == 0 else part + 1, part + 2):
-            for offset in order:
-                block_copy(message, offset).wait_recv()
+        with jax.named_scope(f"wait_{part}"):
+            for message in range(0 if part == 0 else part + 1, part + 2):
+                for other in others:
+                    block_copy(message, other, other).wait_recv()
+        if part + AHEAD <= parts:
+            send_all(part + AHEAD)
 
         def gathered(block):
             return arrived[:, block].reshape(dates, LANES)
@@ -244,13 +291,14 @@
             real, imag = window_coherence(dot_nt(left, right), looks_count)
             coherence_ref[0, 0, 0, window] = real
             coherence_ref[1, 0, 0, window] = imag
-            matrices.append(jnp.concatenate([real, imag], axis=0))
+            matrices.append(jnp.concatenate([real, imag], axis=1))
         for inner, (real, imag) in enumerate(link_windows(matrices)):
             vectors[0, pl.ds(part * QUAD + inner, 1)] = real
             vectors[1, pl.ds(part * QUAD + inner, 1)] = imag
 
     for part in range(parts):
-        compute_part(part)
+        with jax.named_scope(f"part_{part}"):
+            compute_part(part)
 
     fold, rows, width = own // turned.shape[1], turned.shape[1], 2 * windows
     spread = jnp.concatenate([vectors[0], vectors[1]], axis=0)
@@ -262,22 +310,22 @@
         ).reshape(count, rows, LANES)
     turned[...] = folded
 
-    def back_copy(offset):
-        other = lax.rem(me + offset, count)
+    def back_copy(other, source):
         return pltpu.make_async_remote_copy(
             src_ref=turned.at[other],
-            dst_ref=landed.at[me],
-            send_sem=back_send.at[offset],
-            recv_sem=back_recv.at[offset],
+            dst_ref=landed.at[source],
+            send_sem=back_send.at[other],
+            recv_sem=back_recv.at[source],
             device_id={"date": other},
             device_id_type=pl.DeviceIdType.MESH,
         )
 
-    for offset in range(1, count):
-        back_copy(offset).start()
+    for other in reversed(others):
+        back_copy(other, me).start()
     landed[me] = turned[me]
-    for offset in range(1, count):
-        back_copy(offset).wait_recv()
+    with jax.named_scope("wait_back"):
+        for other in others:
+            back_copy(other, other).wait_recv()
     for side in range(2):
         for place in range(fold):
             first = place * width + side * windows
@@ -286,10 +334,10 @@
             )
 
     for message in range(parts + 1):
-        for offset in range(1, count):
-            block_copy(message, offset).wait_send()
-    for offset in range(1, count):
-        back_copy(offset).wait_send()
+        for other in others:
+            block_copy(message, other, me).wait_send()
+    for other in others:
+        back_copy(other, me).wait_send()
 
 
 def deliver(coherence_in, linked_in, coherence_out, linked_out, sem):
@@ -349,6 +397,7 @@
             pltpu.SemaphoreType.DMA((parts + 1, count)),
             pltpu.SemaphoreType.DMA((count,)),
             pltpu.SemaphoreType.DMA((count,)),
+            pltpu.SemaphoreType.REGULAR((count // PAIR + PAIR - 2,)),
         ],
         compiler_params=pltpu.CompilerParams(collective_id=0, has_side_effects=True, vmem_limit_bytes=24 << 20),
     )(pltpu.with_memory_space_constraint(slc, pltpu.HBM), pltpu.with_memory_space_constraint(usable, pltpu.HBM))

time: 33.8 us -> 32.9 us (0.973)
  Pallas kernels: 33 us -> 32.2 us
    pallas_call x1, Pallas kernels: 32 us -> 31.1 us  [local(): pl.pallas_call(functools.partial(kernel, count, looks_count, per_device),...]
where the time goes in v3:
time: 32.9 us; the launch traced here: 32.8 us
  Pallas kernels  32.2 us (98%)
  between operations  0.64 us (2%)
    pallas_call x1, Pallas kernels, local(): pl.pallas_call(functools.partial(kernel, count, looks_count, per_device),...  31.1 us
    pallas_call x1, Pallas kernels, local(): pl.pallas_call(deliver, out_shape=tuple((jax.ShapeDtypeStruct(array.shape...  1.01 us

profile of v3, /device:TPU:0, one launch (start us, length us, event | category | flops | bytes accessed | tf_op | source)
XLA Modules:
  0.0 32.8 jit_solution(10575919115990994551)
XLA Ops:
  0.6 31.1 %shard_map.41 = (bf16[2,1,1,16,128,128]{5,4,3,2,1,0:T(8,128)(2,1)S(1)}, f32[2,16,128]{2,1,0:T(8,128)S(1)}) custom-call(bf16[2,100,16,128]{3,2,1,0:T(8,128)(2,1)} %slc_hbm.1, s32[100,16,128]{2,1,0:T(8,128)} %usable_hbm.1), custom_call_target="tpu_custom_call" | custom-call | tf_op jit(solution)/shard_map/pallas_call | solution.py:376
  31.8 1.0 %shard_map.42 = (bf16[2,1,1,16,128,128]{5,4,3,2,1,0:T(8,128)(2,1)}, f32[2,16,128]{2,1,0:T(8,128)}) custom-call(bf16[2,1,1,16,128,128]{5,4,3,2,1,0:T(8,128)(2,1)S(1)} %get-tuple-element.4.coherence_in, f32[2,16,128]{2,1,0:T(8,128)S(1)} %get-tuple-element.5.linked_in), custom_call_target="tpu_custom_call" | custom-call | tf_op jit(solution)/shard_map/pallas_call | solution.py:404

commit v4 on v3

--- a/solution.py
+++ b/solution.py
@@ -11,7 +11,7 @@
 LANES = 128
 QUAD = 4
 PAIR = 2
-AHEAD = 3
+SENT = ((4, 5), (2, 4, 5))
 PIECES = 2
 NT = (((1,), (1,)), ((), ()))
 
@@ -126,6 +126,7 @@
     in_sem, send_sem, recv_sem, back_send, back_recv, round_sem,
 ):
     me = lax.axis_index("date")
+    core = jnp.minimum(lax.axis_index("sub"), len(SENT) - 1)
     own, local_windows = usable_ref.shape[1:]
     dates = count * own
     span = LANES // QUAD
@@ -252,8 +253,17 @@
         if distance < farthest:
             greet(round_sem.at[distance - 1])
         send_at(distance, [0, 1])
-    for message in range(2, min(AHEAD, parts + 1)):
-        send_all(message)
+    def send_paced(arrived_parts):
+        for index, counts in enumerate(SENT):
+            first = counts[min(arrived_parts - 1, len(counts) - 1)] if arrived_parts else 2
+            messages = range(first, min(counts[min(arrived_parts, len(counts) - 1)], parts + 1))
+            if messages:
+                @pl.when(core == index)
+                def _():
+                    for message in messages:
+                        send_all(message)
+
+    send_paced(0)
     arrived[me] = packed[me]
 
     lane = lax.broadcasted_iota(jnp.int32, (2 * dates, LANES), 1)
@@ -263,8 +273,7 @@
             for message in range(0 if part == 0 else part + 1, part + 2):
                 for other in others:
                     block_copy(message, other, other).wait_recv()
-        if part + AHEAD <= parts:
-            send_all(part + AHEAD)
+        send_paced(part + 1)
 
         def gathered(block):
             return arrived[:, block].reshape(dates, LANES)

time: 32.9 us -> 31.7 us (0.964)
  the two profiles are of different devices: /device:TPU:0 before, /device:TPU:1 now
where the time goes in v4:
time: 31.7 us; the launch traced here: 31.6 us
  Pallas kernels  31 us (98%)
  between operations  0.64 us (2%)
    pallas_call x1, Pallas kernels, local(): pl.pallas_call(functools.partial(kernel, count, looks_count, per_device),...  30 us
    pallas_call x1, Pallas kernels, local(): pl.pallas_call(deliver, out_shape=tuple((jax.ShapeDtypeStruct(array.shape...  1.01 us

profile of v4, /device:TPU:1, one launch (start us, length us, event | category | flops | bytes accessed | tf_op | source)
XLA Modules:
  0.0 31.6 jit_solution(10986366594775305379)
XLA Ops:
  0.6 30.0 %shard_map.41 = (bf16[2,1,1,16,128,128]{5,4,3,2,1,0:T(8,128)(2,1)S(1)}, f32[2,16,128]{2,1,0:T(8,128)S(1)}) custom-call(bf16[2,100,16,128]{3,2,1,0:T(8,128)(2,1)} %slc_hbm.1, s32[100,16,128]{2,1,0:T(8,128)} %usable_hbm.1), custom_call_target="tpu_custom_call" | custom-call | tf_op jit(solution)/shard_map/pallas_call | solution.py:385
  30.6 1.0 %shard_map.42 = (bf16[2,1,1,16,128,128]{5,4,3,2,1,0:T(8,128)(2,1)}, f32[2,16,128]{2,1,0:T(8,128)}) custom-call(bf16[2,1,1,16,128,128]{5,4,3,2,1,0:T(8,128)(2,1)S(1)} %get-tuple-element.4.coherence_in, f32[2,16,128]{2,1,0:T(8,128)S(1)} %get-tuple-element.5.linked_in), custom_call_target="tpu_custom_call" | custom-call | tf_op jit(solution)/shard_map/pallas_call | solution.py:413

commit v5 on v4

--- a/solution.py
+++ b/solution.py
@@ -11,6 +11,7 @@
 LANES = 128
 QUAD = 4
 PAIR = 2
+
 SENT = ((4, 5), (2, 4, 5))
 PIECES = 2
 NT = (((1,), (1,)), ((), ()))
@@ -44,10 +45,14 @@
     return blocks
 
 
-def window_coherence(sums, looks_count):
+def cross_sums(left, right):
+    sums = dot_nt(left, right)
     dates = sums.shape[0] // 2
-    real_sum = sums[:dates, :dates] + sums[dates:, dates:]
-    imag_sum = sums[dates:, :dates] - sums[:dates, dates:]
+    return sums[:dates, :dates] + sums[dates:, dates:], sums[dates:, :dates] - sums[:dates, dates:]
+
+
+def window_coherence(real_sum, imag_sum, looks_count):
+    dates = real_sum.shape[0]
     rows = lax.broadcasted_iota(jnp.int32, (dates, dates), 0)
     columns = lax.broadcasted_iota(jnp.int32, (dates, dates), 1)
     diagonal = jnp.where(rows == columns, real_sum, 0.0)
@@ -64,29 +69,31 @@
     is_imag = jnp.logical_and(row >= 3, row < 6)
     is_first = jnp.logical_or(row == 0, row == 3)
     is_second = jnp.logical_or(row == 1, row == 4)
-    state = [jnp.where(is_real, 1.0, 0.0)] * len(matrices)
-    scales = [None] * len(matrices)
+    state, scales = [None] * len(matrices), [None] * len(matrices)
     result = []
     for step in range(ITERS):
-        products = []
-        for vec, matrix in zip(state, matrices):
+        products = [None] * len(matrices)
+        for index, (vec, matrix) in enumerate(zip(state, matrices) if step else ()):
             high = vec.astype(jnp.bfloat16).astype(jnp.float32)
             left = vec - high
             middle = left.astype(jnp.bfloat16).astype(jnp.float32)
             pieces = jnp.where(is_first, high, jnp.where(is_second, middle, left - middle))
-            products.append(jnp.dot(pieces.astype(jnp.bfloat16), matrix, preferred_element_type=jnp.float32))
+            products[index] = jnp.dot(pieces.astype(jnp.bfloat16), matrix, preferred_element_type=jnp.float32)
         for index, product in enumerate(products):
-            first, second = product[:, :dates], product[:, dates:]
-            zero = jnp.zeros_like(first)
-            new_real = jnp.sum(
-                jnp.where(is_real, first, jnp.where(is_imag, second, zero)), axis=0, keepdims=True
-            )
-            new_imag = jnp.sum(
-                jnp.where(is_real, -second, jnp.where(is_imag, first, zero)), axis=0, keepdims=True
-            )
             if step:
+                first, second = product[:, :dates], product[:, dates:]
+                zero = jnp.zeros_like(first)
+                new_real = jnp.sum(
+                    jnp.where(is_real, first, jnp.where(is_imag, second, zero)), axis=0, keepdims=True
+                )
+                new_imag = jnp.sum(
+                    jnp.where(is_real, -second, jnp.where(is_imag, first, zero)), axis=0, keepdims=True
+                )
                 new_real = new_real * scales[index]
                 new_imag = new_imag * scales[index]
+            else:
+                sums = jnp.sum(matrices[index].astype(jnp.float32), axis=0, keepdims=True)
+                new_real, new_imag = sums[:, :dates], -sums[:, dates:]
             power = jnp.sum(new_real * new_real + new_imag * new_imag, axis=1, keepdims=True)
             scales[index] = lax.rsqrt(power * (1.0 / dates) + 1e-05)
             if step == ITERS - 1:
@@ -123,7 +130,7 @@
     count, looks_count, windows,
     slc_hbm, usable_hbm, coherence_ref, linked_ref,
     slc_ref, usable_ref, packed, arrived, vectors, turned, landed,
-    in_sem, send_sem, recv_sem, back_send, back_recv, round_sem,
+    in_sem, send_sem, recv_sem, back_send, back_recv, round_sem, partial,
 ):
     me = lax.axis_index("date")
     core = jnp.minimum(lax.axis_index("sub"), len(SENT) - 1)
@@ -233,7 +240,7 @@
                     block_copy(message, other, me).start()
 
     def send_all(message):
-        for other in others:
+        for other in others if message == parts else reversed(others):
             block_copy(message, other, me).start()
 
     with jax.named_scope("prepare_first"):
@@ -268,36 +275,53 @@
 
     lane = lax.broadcasted_iota(jnp.int32, (2 * dates, LANES), 1)
 
-    def compute_part(part):
+    def gathered(block):
+        return arrived[:, block].reshape(dates, LANES)
+
+    def shared_columns():
+        columns = []
+        for piece in range(extra):
+            both = gathered(2 * parts + piece)
+            columns.append((jnp.concatenate([both, pltpu.roll(both, LANES // 2, 1)], axis=0), True))
+        return columns
+
+    def span_columns(part, spans):
+        columns = []
+        for index in spans:
+            sides = [
+                gathered(later_block(part, side, index) if index else first_block(part, side)) for side in range(2)
+            ]
+            columns.append((jnp.concatenate(sides, axis=0), False))
+        return columns
+
+    def windows_sums(part, columns):
+        right = jnp.concatenate([block for block, _ in columns], axis=1)
+        for inner in range(QUAD):
+            mine = jnp.logical_and(lane < LANES // 2, (lane & (windows - 1)) == part * QUAD + inner)
+            own_lane = (lane & (QUAD - 1)) == inner
+            left = jnp.concatenate(
+                [jnp.where(mine if shared else own_lane, block, jnp.zeros_like(block)) for block, shared in columns],
+                axis=1,
+            )
+            yield cross_sums(left, right)
+
+    def sum_ahead(part):
+        for inner, sums in enumerate(windows_sums(part, shared_columns() + span_columns(part, [0]))):
+            partial[inner, 0], partial[inner, 1] = sums
+
+    def compute_part(part, ahead):
         with jax.named_scope(f"wait_{part}"):
             for message in range(0 if part == 0 else part + 1, part + 2):
                 for other in others:
                     block_copy(message, other, other).wait_recv()
         send_paced(part + 1)
-
-        def gathered(block):
-            return arrived[:, block].reshape(dates, LANES)
-
-        columns = []
-        for piece in range(extra):
-            both = gathered(2 * parts + piece)
-            columns.append((jnp.concatenate([both, pltpu.roll(both, LANES // 2, 1)], axis=0), True))
-        for index in range(full):
-            sides = [
-                gathered(later_block(part, side, index) if index else first_block(part, side)) for side in range(2)
-            ]
-            columns.append((jnp.concatenate(sides, axis=0), False))
-        right = jnp.concatenate([block for block, _ in columns], axis=1)
+        columns = span_columns(part, range(1, full)) if ahead else shared_columns() + span_columns(part, range(full))
         matrices = []
-        for inner in range(QUAD):
+        for inner, (real_sum, imag_sum) in enumerate(windows_sums(part, columns)):
             window = part * QUAD + inner
-            mine = jnp.logical_and(lane < LANES // 2, (lane & (windows - 1)) == window)
-            own_lane = (lane & (QUAD - 1)) == inner
-            left = jnp.concatenate(
-                [jnp.where(mine if shared else own_lane, block, jnp.zeros_like(block)) for block, shared in columns],
-                axis=1,
-            )
-            real, imag = window_coherence(dot_nt(left, right), looks_count)
+            if ahead:
+                real_sum, imag_sum = real_sum + partial[inner, 0], imag_sum + partial[inner, 1]
+            real, imag = window_coherence(real_sum, imag_sum, looks_count)
             coherence_ref[0, 0, 0, window] = real
             coherence_ref[1, 0, 0, window] = imag
             matrices.append(jnp.concatenate([real, imag], axis=1))
@@ -307,7 +331,10 @@
 
     for part in range(parts):
         with jax.named_scope(f"part_{part}"):
-            compute_part(part)
+            ahead = 0 < part == parts - 1 and full > 1
+            if ahead:
+                sum_ahead(part)
+            compute_part(part, ahead)
 
     fold, rows, width = own // turned.shape[1], turned.shape[1], 2 * windows
     spread = jnp.concatenate([vectors[0], vectors[1]], axis=0)
@@ -407,6 +434,7 @@
             pltpu.SemaphoreType.DMA((count,)),
             pltpu.SemaphoreType.DMA((count,)),
             pltpu.SemaphoreType.REGULAR((count // PAIR + PAIR - 2,)),
+            pltpu.VMEM((QUAD, 2, dates, dates), jnp.float32),
         ],
         compiler_params=pltpu.CompilerParams(collective_id=0, has_side_effects=True, vmem_limit_bytes=24 << 20),
     )(pltpu.with_memory_space_constraint(slc, pltpu.HBM), pltpu.with_memory_space_constraint(usable, pltpu.HBM))

time: 31.7 us -> 30.9 us (0.975)
  the two profiles are of different devices: /device:TPU:1 before, /device:TPU:0 now
where the time goes in v5:
time: 30.9 us; the launch traced here: 30.6 us
  Pallas kernels  29.9 us (97%)
  between operations  0.64 us (2%)
    pallas_call x1, Pallas kernels, local(): pl.pallas_call(functools.partial(kernel, count, looks_count, per_device),...  28.9 us
    pallas_call x1, Pallas kernels, local(): pl.pallas_call(deliver, out_shape=tuple((jax.ShapeDtypeStruct(array.shape...  1.01 us

profile of v5, /device:TPU:0, one launch (start us, length us, event | category | flops | bytes accessed | tf_op | source)
XLA Modules:
  0.0 30.6 jit_solution(14482890051611479828)
XLA Ops:
  0.6 28.9 %shard_map.41 = (bf16[2,1,1,16,128,128]{5,4,3,2,1,0:T(8,128)(2,1)S(1)}, f32[2,16,128]{2,1,0:T(8,128)S(1)}) custom-call(bf16[2,100,16,128]{3,2,1,0:T(8,128)(2,1)} %slc_hbm.1, s32[100,16,128]{2,1,0:T(8,128)} %usable_hbm.1), custom_call_target="tpu_custom_call" | custom-call | tf_op jit(solution)/shard_map/pallas_call | solution.py:412
  29.6 1.0 %shard_map.42 = (bf16[2,1,1,16,128,128]{5,4,3,2,1,0:T(8,128)(2,1)}, f32[2,16,128]{2,1,0:T(8,128)}) custom-call(bf16[2,1,1,16,128,128]{5,4,3,2,1,0:T(8,128)(2,1)S(1)} %get-tuple-element.4.coherence_in, f32[2,16,128]{2,1,0:T(8,128)S(1)} %get-tuple-element.5.linked_in), custom_call_target="tpu_custom_call" | custom-call | tf_op jit(solution)/shard_map/pallas_call | solution.py:441

commit v6 on v5

--- a/solution.py
+++ b/solution.py
@@ -240,7 +240,7 @@
                     block_copy(message, other, me).start()
 
     def send_all(message):
-        for other in others if message == parts else reversed(others):
+        for other in others if message >= parts - 1 else reversed(others):
             block_copy(message, other, me).start()
 
     with jax.named_scope("prepare_first"):

time: 30.9 us -> 30.9 us (level)
  no operation moved by 1% of the time
where the time goes in v6:
time: 30.9 us; the launch traced here: 30.6 us
  Pallas kernels  30 us (97%)
  between operations  0.64 us (2%)
    pallas_call x1, Pallas kernels, local(): pl.pallas_call(functools.partial(kernel, count, looks_count, per_device),...  29 us
    pallas_call x1, Pallas kernels, local(): pl.pallas_call(deliver, out_shape=tuple((jax.ShapeDtypeStruct(array.shape...  1.01 us

profile of v6, /device:TPU:0, one launch (start us, length us, event | category | flops | bytes accessed | tf_op | source)
XLA Modules:
  0.0 30.6 jit_solution(9184156115531704487)
XLA Ops:
  0.6 29.0 %shard_map.41 = (bf16[2,1,1,16,128,128]{5,4,3,2,1,0:T(8,128)(2,1)S(1)}, f32[2,16,128]{2,1,0:T(8,128)S(1)}) custom-call(bf16[2,100,16,128]{3,2,1,0:T(8,128)(2,1)} %slc_hbm.1, s32[100,16,128]{2,1,0:T(8,128)} %usable_hbm.1), custom_call_target="tpu_custom_call" | custom-call | tf_op jit(solution)/shard_map/pallas_call | solution.py:412
  29.6 1.0 %shard_map.42 = (bf16[2,1,1,16,128,128]{5,4,3,2,1,0:T(8,128)(2,1)}, f32[2,16,128]{2,1,0:T(8,128)}) custom-call(bf16[2,1,1,16,128,128]{5,4,3,2,1,0:T(8,128)(2,1)S(1)} %get-tuple-element.4.coherence_in, f32[2,16,128]{2,1,0:T(8,128)S(1)} %get-tuple-element.5.linked_in), custom_call_target="tpu_custom_call" | custom-call | tf_op jit(solution)/shard_map/pallas_call | solution.py:441
